TPU v7x, 32 devices: a whole 2x2x4 slice. The times are simulated.
32 devices in a mesh: fsdp: 32 (over z, y, x, core).
Axes of the slice: x: 2, y: 2, z: 4, core: 2. Of those that a mesh axis runs over, the one named last changes fastest.
Arguments:
- images: bfloat16 [2, 64, 197, 384], P(None, 'fsdp'), may hold values from -6 to 6
- cotangent: bfloat16 [2, 64, 197, 384], P(None, 'fsdp'), may hold values from -6 to 6
- counts: int32 [2, 32], P(None, 'fsdp'), may hold values from 1 to 2, as said below
- master: float32 [2, 1777664], P(None, 'fsdp'), may hold values from -10 to 10, as said below
- moment_one: float32 [2, 1777664], P(None, 'fsdp'), may hold values from -0.3125 to 0.3125
- moment_two: float32 [2, 1777664], P(None, 'fsdp'), may hold values from 1e-06 to 0.0001
Outputs:
- activations: bfloat16 [2, 64, 197, 384], P(None, 'fsdp')
- input_grad: float32 [2, 64, 197, 384], P(None, 'fsdp')
- weight_grad: float32 [2, 1777664], P(None, 'fsdp')
- new_master: float32 [2, 1777664], P(None, 'fsdp')
- new_moment_one: float32 [2, 1777664], P(None, 'fsdp')
- new_moment_two: float32 [2, 1777664], P(None, 'fsdp')
Inputs may be any that keep to these rules, and one draw needn't show every extreme that they name: `counts`: each device has one or two live slots in every micro-batch; in every micro-batch some device has two and some has one. `master`: gains lie near one; biases and matrix entries are bounded.
All inputs are finite; a program needn't handle non-finite values.
Results may differ from a plain program's by a relative error of at most 0.017.
Values may be sent and summed in bfloat16 or wider, within the bound.
A program may use at most 256 MiB of HBM per device.

v0:
```python
import functools
import math

import jax
import jax.numpy as jnp
from jax import lax
from jax.experimental import pallas as pl
from jax.experimental.pallas import tpu as pltpu
from jax.sharding import PartitionSpec as P

D = 384
H = 6
HD = 64
FF = 1536
SEQ = 197
STEP = 3
TP = 208
QP = 256

beta_one = 0.9
beta_two = 0.999
learn_rate = 0.05
decay_rate = 0.05
epsilon = 1e-08

f32 = jnp.float32
bf = jnp.bfloat16
R_QKV, R_P, R_U, R_D, R_END = 36, 3492, 4644, 9252, 13860
NN = (((1,), (0,)), ((), ()))
NT = (((1,), (1,)), ((), ()))
TN = (((0,), (0,)), ((), ()))
G1, B1, BQ, BV, BP, G2, B2, BD, BU = range(9)


def dot(a, b, dims):
    return lax.dot_general(a, b, dims, preferred_element_type=f32)


def wide(r):
    return jnp.concatenate([r, r, r], axis=1)


def rowsum(x):
    return jnp.sum(x, 0, keepdims=True)


def norm(x):
    m = jnp.sum(x, -1, keepdims=True) * (1.0 / D)
    c = x - m
    v = jnp.sum(c * c, -1, keepdims=True) * (1.0 / D)
    r = lax.rsqrt(v + 1e-6)
    return c * r, jnp.broadcast_to(r, (x.shape[0], 128))


def norm_back(dh, n, r, g, dy):
    e = dh * g
    me = jnp.sum(e, -1, keepdims=True) * (1.0 / D)
    men = jnp.sum(e * n, -1, keepdims=True) * (1.0 / D)
    return dy + (e - me - n * men) * wide(r)


def half_mask(rows, e):
    lane = lax.broadcasted_iota(jnp.int32, (rows, 128), 1)
    return (lane < 64) if e == 0 else (lane >= 64)


def keep(mask, v):
    return jnp.where(mask, v, jnp.zeros_like(v))


class NS:
    pass


SAVED = [
    ("N1", (TP, D), bf),
    ("R1", (TP, 128), f32),
    ("Q", (QP, D), bf),
    ("KV", (TP, 2 * D), bf),
    ("PT", (H, TP, QP), bf),
    ("O", (TP, D), bf),
    ("N2", (TP, D), bf),
    ("R2", (TP, 128), f32),
    ("GB", (TP, FF), bf),
    ("GP", (TP, FF), bf),
]


def unpack_layer(S, l, nd, rows):
    wg, F, V = S.wg.at[l], S.F, S.V.at[l]

    def put(d, c):
        F[pl.ds(rows * d, rows), :] = wg[d, 0:rows, :].astype(f32)
        return c

    lax.fori_loop(0, nd, put, 0)
    for k in range(8):
        for j in range(3):
            V[k : k + 1, 128 * j : 128 * j + 128] = F[3 * k + j : 3 * k + j + 1, :]
    for j in range(12):
        V[8:9, 128 * j : 128 * j + 128] = F[24 + j : 25 + j, :]
    for W, off, h, w in ((S.Wq, R_QKV, D, 3 * D), (S.Wp, R_P, D, D), (S.Wu, R_U, D, FF), (S.Wd, R_D, FF, D)):
        n = w // 128
        for j in range(n):
            W[l, :, 128 * j : 128 * j + 128] = F[pl.ds(off + j, h, stride=n), :].astype(bf)


def fwd_attention(S, l, i):
    V = S.V
    n1, r1 = norm(S.X[i])
    S.N1[l, i] = n1.astype(bf)
    S.R1[l, i] = r1
    h = (n1 * V[l, G1 : G1 + 1, 0:D] + V[l, B1 : B1 + 1, 0:D]).astype(bf)
    qkv = dot(h, S.Wq[l], NN)
    S.Q[l, i, 0:TP, :] = (qkv[:, 0:D] + V[l, BQ : BQ + 1, 0:D]).astype(bf)
    S.KV[l, i, :, 0:D] = qkv[:, D : 2 * D].astype(bf)
    S.KV[l, i, :, D : 2 * D] = (qkv[:, 2 * D :] + V[l, BV : BV + 1, 0:D]).astype(bf)
    row = lax.broadcasted_iota(jnp.int32, (TP, QP), 0)
    for p in range(3):
        kp = S.KV[l, i, :, 128 * p : 128 * p + 128] * jnp.asarray(0.125, bf)
        vp = S.KV[l, i, :, D + 128 * p : D + 128 * p + 128]
        qp = S.Q[l, i, :, 128 * p : 128 * p + 128]
        o = None
        for e in range(2):
            m = half_mask(TP, e)
            s = dot(keep(m, kp), qp, NT)
            s = jnp.where(row < SEQ, s, -1e30)
            ex = jnp.exp(s - jnp.max(s, 0, keepdims=True))
            pb = (ex * (1.0 / jnp.sum(ex, 0, keepdims=True))).astype(bf)
            S.PT[l, i, 2 * p + e] = pb
            oo = dot(pb, keep(m, vp), TN)
            o = oo if o is None else o + oo
        S.O[l, i, :, 128 * p : 128 * p + 128] = o[0:TP].astype(bf)


def fwd_mlp(S, l, i):
    V = S.V
    x1 = S.X[i] + dot(S.O[l, i], S.Wp[l], NN) + V[l, BP : BP + 1, 0:D]
    n2, r2 = norm(x1)
    S.N2[l, i] = n2.astype(bf)
    S.R2[l, i] = r2
    h2 = (n2 * V[l, G2 : G2 + 1, 0:D] + V[l, B2 : B2 + 1, 0:D]).astype(bf)
    for c in range(3):
        sl = slice(512 * c, 512 * c + 512)
        u = dot(h2, S.Wu[l, :, sl], NN) + V[l, BU : BU + 1, sl]
        phi = 0.5 + 0.5 * lax.erf(u * math.sqrt(0.5))
        S.GB[l, i, :, sl] = (u * phi).astype(bf)
        S.GP[l, i, :, sl] = (phi + u * (jnp.exp(u * u * -0.5) * (1.0 / math.sqrt(2 * math.pi)))).astype(bf)
    S.X[i] = x1 + dot(S.GB[l, i], S.Wd[l], NN) + V[l, BD : BD + 1, 0:D]


def bwd_mlp(S, l, i):
    V, VG = S.V, S.VG
    dy = S.DX[i]
    dm = dy.astype(bf)
    S.DM[i] = dm
    VG[BD : BD + 1, 0:D] += rowsum(dy)
    for c in range(3):
        sl = slice(512 * c, 512 * c + 512)
        du = dot(dm, S.Wd[l, sl, :], NT) * S.GP[l, i, :, sl].astype(f32)
        VG[BU : BU + 1, sl] += rowsum(du)
        S.GP[l, i, :, sl] = du.astype(bf)
    dh2 = dot(S.GP[l, i], S.Wu[l], NT)
    n2 = S.N2[l, i].astype(f32)
    VG[G2 : G2 + 1, 0:D] += rowsum(dh2 * n2)
    VG[B2 : B2 + 1, 0:D] += rowsum(dh2)
    dx1 = norm_back(dh2, n2, S.R2[l, i], V[l, G2 : G2 + 1, 0:D], dy)
    VG[BP : BP + 1, 0:D] += rowsum(dx1)
    S.DA[i] = dx1.astype(bf)
    S.DX[i] = dx1


def bwd_attention(S, l, i):
    V, VG = S.V, S.VG
    S.DO[0:TP, :] = dot(S.DA[i], S.Wp[l], NT).astype(bf)
    eighth = jnp.asarray(0.125, bf)
    for p in range(3):
        kp = S.KV[l, i, :, 128 * p : 128 * p + 128] * eighth
        vp = S.KV[l, i, :, D + 128 * p : D + 128 * p + 128]
        qp = S.Q[l, i, :, 128 * p : 128 * p + 128] * eighth
        do = S.DO[:, 128 * p : 128 * p + 128]
        dq = dk = dv = None
        for e in range(2):
            m = half_mask(TP, e)
            mq = half_mask(QP, e)
            pb = S.PT[l, i, 2 * p + e]
            dp = dot(keep(m, vp), do, NT)
            pf = pb.astype(f32)
            t = pf * dp
            ds = (t - pf * rowsum(t)).astype(bf)
            a = dot(pb, keep(mq, do), NN)
            b = dot(ds, keep(mq, qp), NN)
            c = dot(ds, keep(m, kp), TN)
            dv = a if dv is None else dv + a
            dk = b if dk is None else dk + b
            dq = c if dq is None else dq + c
        dq = dq[0:TP]
        sl = slice(128 * p, 128 * p + 128)
        VG[BQ : BQ + 1, sl] += rowsum(dq)
        VG[BV : BV + 1, sl] += rowsum(dv)
        S.DQKV[i, :, sl] = dq.astype(bf)
        S.DQKV[i, :, D + 128 * p : D + 128 * p + 128] = dk.astype(bf)
        S.DQKV[i, :, 2 * D + 128 * p : 2 * D + 128 * p + 128] = dv.astype(bf)
    dh = dot(S.DQKV[i], S.Wq[l], NT)
    n1 = S.N1[l, i].astype(f32)
    VG[G1 : G1 + 1, 0:D] += rowsum(dh * n1)
    VG[B1 : B1 + 1, 0:D] += rowsum(dh)
    S.DX[i] = norm_back(dh, n1, S.R1[l, i], V[l, G1 : G1 + 1, 0:D], S.DX[i])


def flat(v):
    return v.reshape(v.shape[0] * v.shape[1], v.shape[2])


def store_grad(F, val, first, n):
    for j in range(val.shape[1] // 128):
        F[pl.ds(first + j, val.shape[0], stride=n), :] = val[:, 128 * j : 128 * j + 128]


def grads_mlp(S, l):
    V, F = S.V, S.F
    dm = flat(S.DM[...])
    for c in range(3):
        gb = flat(S.GB[l, :, :, 512 * c : 512 * c + 512])
        store_grad(F, dot(gb, dm, TN), R_D + 3 * 512 * c, 3)
    h2 = (flat(S.N2[l]).astype(f32) * V[l, G2 : G2 + 1, 0:D] + V[l, B2 : B2 + 1, 0:D]).astype(bf)
    for c in range(3):
        du = flat(S.GP[l, :, :, 512 * c : 512 * c + 512])
        store_grad(F, dot(h2, du, TN), R_U + 4 * c, 12)


def grads_attention(S, l):
    V, VG, F = S.V, S.VG, S.F
    store_grad(F, dot(flat(S.O[l]), flat(S.DA[...]), TN), R_P, 3)
    h = (flat(S.N1[l]).astype(f32) * V[l, G1 : G1 + 1, 0:D] + V[l, B1 : B1 + 1, 0:D]).astype(bf)
    for c0, c1 in ((0, 512), (512, 1024), (1024, 1152)):
        store_grad(F, dot(h, flat(S.DQKV[:, :, c0:c1]), TN), R_QKV + c0 // 128, 9)
    for k in range(8):
        for j in range(3):
            F[3 * k + j : 3 * k + j + 1, :] = VG[k : k + 1, 128 * j : 128 * j + 128]
    for j in range(12):
        F[24 + j : 25 + j, :] = VG[8:9, 128 * j : 128 * j + 128]


def topology(mesh):
    devices = list(mesh.devices.flat)
    where = {}
    for index, device in enumerate(devices):
        where[tuple(device.coords) + (device.core_on_chip,)] = index
    sizes = [max(key[a] for key in where) - min(key[a] for key in where) + 1 for a in range(4)]
    origin = [min(key[a] for key in where) for a in range(4)]
    dims = []
    for a in range(4):
        if sizes[a] > 1:
            step = list(origin)
            step[a] += 1
            dims.append((int(sizes[a]), int(where[tuple(step)] - where[tuple(origin)])))
        else:
            dims.append((1, 1))
    for key, index in where.items():
        assert index == sum((key[a] - origin[a]) * dims[a][1] for a in range(4))
    chip = sorted(dims[:3], key=lambda d: -d[0])
    return tuple(chip) + (dims[3],)


class Net:
    def __init__(self, topo):
        self.topo = topo
        self.me = lax.axis_index("fsdp")
        self.at = [lax.rem(lax.div(self.me, stride), size) for size, stride in topo]

    def move(self, index, axis, by):
        size, stride = self.topo[axis]
        if by == 0 or size == 1:
            return index
        return index + (lax.rem(self.at[axis] + by, size) - self.at[axis]) * stride

    def block(self, offsets):
        index = self.me
        for axis, by in offsets.items():
            index = self.move(index, axis, by)
        return index

    def peers(self):
        out = []
        for axis, (size, _) in enumerate(self.topo):
            out += [self.move(self.me, axis, by) for by in range(1, size)]
        return out


def remote(src, dst, send, recv, peer):
    return pltpu.make_async_remote_copy(
        src_ref=src, dst_ref=dst, send_sem=send, recv_sem=recv, device_id=(peer,), device_id_type=pl.DeviceIdType.MESH
    )


def halves(RP):
    first = 16 * ((RP // 16 + 1) // 2)
    return ((0, first), (first, RP - first))


def gather_events(net, wg, send, recv):
    RP = wg.shape[1]
    cut = halves(RP)
    nz, n1, n2, nc = [size for size, _ in net.topo]
    orders = ((1, 2), (2, 1))

    def copy(c, blk, peer):
        first, count = cut[c]
        ref = wg.at[blk, pl.ds(first, count), :]
        return remote(ref, ref, send, recv.at[c, blk], peer)

    def targets(axes):
        return [net.move(net.me, axis, by) for axis in axes for by in range(1, net.topo[axis][0])]

    def forward(c, blk, axes):
        for peer in targets(axes):
            copy(c, blk, peer).start()

    def arrived(c, blk, axes):
        ends = targets(axes)

        def run():
            copy(c, blk, net.me).wait_recv()
            for peer in ends:
                copy(c, blk, peer).start()

        return run

    events = []

    def start():
        for c in range(2):
            forward(c, net.me, (0,))
        for c in range(2):
            forward(c, net.me, orders[c])
        for c in range(2):
            forward(c, net.me, (3,))

    events.append((-1.0, start))
    for c in range(2):
        P, Q = orders[c]
        sp, sq = net.topo[P][0], net.topo[Q][0]
        for k in range(nz):
            if k:
                events.append((k, arrived(c, net.block({0: k}), (P, Q, 3))))
            for jp in range(1, sp):
                events.append((k + 1.1, arrived(c, net.block({0: k, P: jp}), (Q, 3))))
            for jq in range(1, sq):
                events.append((k + 1.2, arrived(c, net.block({0: k, Q: jq}), (3,))))
                for jp in range(1, sp):
                    events.append((k + 2.3, arrived(c, net.block({0: k, P: jp, Q: jq}), (3,))))
        for k in range(nz):
            for a in range(n1):
                for b in range(n2):
                    for w in range(1, nc):
                        blk = net.block({0: k, 1: a, 2: b, 3: w})
                        events.append((99.0, arrived(c, blk, ())))
    events.sort(key=lambda e: e[0])
    return [e[1] for e in events]


def wait_sends(buf, send, blocks):
    ref = buf.at[pl.ds(0, blocks)]
    pltpu.make_async_copy(ref, ref, send).wait()


def scatter_events(net, G, RB, send, recv):
    RP = G.shape[1]
    cut = halves(RP)
    nz, n1, n2, nc = [size for size, _ in net.topo]
    orders = ((2, 1), (1, 2))
    pending = []

    def flush():
        for start in pending:
            start()
        del pending[:]

    def rows(c):
        return pl.ds(cut[c][0], cut[c][1])

    def add(ref, blk, c):
        G[blk, rows(c), :] = G[blk, rows(c), :] + ref[...]

    def place(off, axis):
        return lax.rem(net.at[axis] + off[axis], net.topo[axis][0])

    def core_sum(off):
        blk = net.block(off)
        s = (place(off, 0) * n1 + place(off, 1)) * n2 + place(off, 2)
        sends = []
        for c in range(2):
            Q, P = orders[c]
            by = off[Q]
            if by:
                spot = place(off, 0) * net.topo[P][0] + place(off, P)
                peer = net.move(net.me, Q, by)
                sends.append((c, by - 1, spot, peer))

        def run():
            for w in range(1, nc):
                remote(RB[0].at[w - 1, s], RB[0].at[w - 1, s], send, recv[0].at[w - 1, s], net.me).wait_recv()
            for c in range(2):
                for w in range(1, nc):
                    add(RB[0].at[w - 1, s, rows(c), :], blk, c)
            flush()
            for c, by, spot, peer in sends:
                pending.append(lambda c=c, by=by, spot=spot, peer=peer: remote(
                    G.at[blk, rows(c), :], RB[1][c].at[by, spot], send, recv[1][c].at[by, spot], peer).start())

        return run

    def second(c, off):
        Q, P = orders[c]
        blk = net.block(off)
        at_z = place(off, 0)
        spot = at_z * net.topo[P][0] + place(off, P)
        by = off[P]
        peer = net.move(net.me, P, by)

        def run():
            for j in range(net.topo[Q][0] - 1):
                ref = RB[1][c].at[j, spot]
                remote(ref, ref, send, recv[1][c].at[j, spot], net.me).wait_recv()
                add(ref, blk, c)
            flush()
            if by:
                pending.append(lambda: remote(
                    G.at[blk, rows(c), :], RB[2][c].at[by - 1, at_z], send, recv[2][c].at[by - 1, at_z], peer).start())

        return run

    def third(c, off):
        Q, P = orders[c]
        blk = net.block(off)
        at_z = place(off, 0)
        by = off[0]
        peer = net.move(net.me, 0, by)

        def run():
            for j in range(net.topo[P][0] - 1):
                ref = RB[2][c].at[j, at_z]
                remote(ref, ref, send, recv[2][c].at[j, at_z], net.me).wait_recv()
                add(ref, blk, c)
            flush()
            if by:
                pending.append(lambda: remote(
                    G.at[blk, rows(c), :], RB[3][c].at[by - 1], send, recv[3][c].at[by - 1], peer).start())

        return run

    def last():
        flush()
        for c in range(2):
            for by in range(1, nz):
                ref = RB[3][c].at[by - 1]
                remote(ref, ref, send, recv[3][c].at[by - 1], net.me).wait_recv()

    events = []
    z_order = [k for k in range(1, nz)] + [0]
    plane = sorted(((a, b) for a in range(n1) for b in range(n2)), key=lambda ab: -((ab[0] > 0) + (ab[1] > 0)))
    for r, k in enumerate(z_order):
        for a, b in plane:
            events.append((r, core_sum({0: k, 1: a, 2: b})))
        for c in range(2):
            Q, P = orders[c]
            for j in list(range(1, net.topo[P][0])) + [0]:
                events.append((r + 1.5 + 0.1 * (j == 0), second(c, {0: k, P: j, Q: 0})))
            events.append((r + 2.7, third(c, {0: k, P: 0, Q: 0})))
    events.sort(key=lambda e: e[0])
    return [e[1] for e in events] + [last], flush


def pack_and_send(net, S, G, RB, send, recv, nd, rows):
    nz, n1, n2, nc = [size for size, _ in net.topo]
    F = S.F

    def chip(t):
        a = lax.div(t, n1 * n2)
        b = lax.rem(lax.div(t, n2), n1)
        g = lax.rem(t, n2)
        base = a * net.topo[0][1] + b * net.topo[1][1] + g * net.topo[2][1]
        return base

    def pack(blk):
        G[blk, 0:rows, :] = F[pl.ds(rows * blk, rows), :].astype(bf)

    def go(t, w):
        blk = chip(t) + lax.rem(net.at[3] + w, nc) * net.topo[3][1]
        remote(G.at[blk], RB[0].at[w - 1, t], send, recv[0].at[w - 1, t], net.move(net.me, 3, w)).start()

    total = nz * n1 * n2
    for w in range(1, nc):
        def step(t, c):
            pack(chip(t) + lax.rem(net.at[3] + w, nc) * net.topo[3][1])

            @pl.when(t > 0)
            def _():
                go(t - 1, w)

            return c

        lax.fori_loop(0, total, step, 0)

    def mine(t, c):
        pack(chip(t) + net.at[3] * net.topo[3][1])
        return c

    lax.fori_loop(0, total, mine, 0)
    for w in range(1, nc):
        go(total - 1, w)


def spread(events, points):
    n = len(events)
    return [events[n * p // points : n * (p + 1) // points] for p in range(points)]


def at_points(groups, index, flush):
    for value, group in enumerate(groups):
        if group:

            @pl.when(index == value)
            def _(group=group):
                for event in group:
                    event()
                flush()


def kernel(cfg, counts, images, cotangent, master, one, two, act, dimg, o_grad, o_master, o_one, o_two, *scr):
    topo, L, NI, nd, rows, slots = cfg
    S = NS()
    for name, ref in zip(NAMES, scr):
        setattr(S, name, ref)
    S.wg = S.wgs
    net = Net(topo)

    barrier = pltpu.get_barrier_semaphore()
    peers = net.peers()
    for peer in peers:
        pl.semaphore_signal(barrier, inc=1, device_id=(peer,), device_id_type=pl.DeviceIdType.MESH)

    loads = [
        pltpu.make_async_copy(master, S.vm, S.lsem.at[0]),
        pltpu.make_async_copy(images, S.vimg, S.lsem.at[1]),
        pltpu.make_async_copy(cotangent, S.vcot, S.lsem.at[2]),
        pltpu.make_async_copy(one, S.v1, S.lsem.at[3]),
        pltpu.make_async_copy(two, S.v2, S.lsem.at[4]),
    ]
    for load in loads:
        load.start()
    loads[0].wait()
    for l in range(L):
        S.wg[l, net.me, 0:rows, :] = S.vm[:, l, :].astype(bf)
    pl.semaphore_wait(barrier, len(peers))

    gathers = [gather_events(net, S.wg.at[l], S.gsend.at[l], S.grecv.at[l]) for l in range(L)]
    split = len(gathers[0])
    gathers[0][0]()

    def live(i):
        return lax.rem(i, slots) < counts[lax.div(i, slots), 0]

    loads[1].wait()
    loads[2].wait()
    edge = SEQ - SEQ % 16

    def init(i, c):
        S.X[i, edge:, :] = jnp.zeros((TP - edge, D), f32)
        S.DX[i, edge:, :] = jnp.zeros((TP - edge, D), f32)
        S.X[i, 0:SEQ, :] = S.vimg[i].astype(f32)
        S.DX[i, 0:SEQ, :] = jnp.where(live(i), S.vcot[i].astype(f32), 0.0)
        for l in range(L):
            S.Q[l, i, TP:, :] = jnp.zeros((QP - TP, D), bf)
        return c

    lax.fori_loop(0, NI, init, 0)
    S.DO[TP:, :] = jnp.zeros((QP - TP, D), bf)

    for event in gathers[0][1:]:
        event()
    unpack_layer(S, 0, nd, rows)

    def nothing():
        pass

    flush = nothing
    for l in range(L):
        groups = []
        if l + 1 < L:
            gathers[l + 1][0]()
            groups = spread(gathers[l + 1][1:], 2 * NI)

        def forward(i, c):
            fwd_attention(S, l, i)
            at_points(groups[0::2], i, flush)
            fwd_mlp(S, l, i)
            at_points(groups[1::2], i, flush)
            return c

        lax.fori_loop(0, NI, forward, 0)
        if l + 1 < L:
            unpack_layer(S, l + 1, nd, rows)

    def finish(i, c):
        S.vimg[i] = jnp.where(live(i), S.X[i, 0:SEQ, :], 0.0).astype(bf)
        return c

    lax.fori_loop(0, NI, finish, 0)
    out_act = pltpu.make_async_copy(S.vimg, act, S.lsem.at[1])
    out_act.start()
    for l in range(L):
        wait_sends(S.wg.at[l], S.gsend.at[l], nd - 1)

    S.F[R_END:, :] = jnp.zeros((nd * rows - R_END, 128), f32)
    RB = [S.rb0, [S.rb1a, S.rb1b], [S.rb2a, S.rb2b], [S.rb3a, S.rb3b]]

    def recv_of(l):
        return [S.rr0.at[l], [S.rr1.at[l, c] for c in range(2)], [S.rr2.at[l, c] for c in range(2)], [S.rr3.at[l, c] for c in range(2)]]

    def adam(l):
        wait_sends(S.wg.at[l], S.rsend.at[l], nd - 1)
        g = []
        for c, (first, count) in enumerate(halves(S.wg.shape[2])):
            part = S.wg[l, net.me, pl.ds(first, count), :].astype(f32)
            for by in range(topo[0][0] - 1):
                part = part + RB[3][c][by].astype(f32)
            g.append(part)
        g = jnp.concatenate(g, axis=0)[0:rows] * (1.0 / (NI * nd))
        m1 = beta_one * S.v1[:, l, :] + (1.0 - beta_one) * g
        m2 = beta_two * S.v2[:, l, :] + (1.0 - beta_two) * g * g
        w = S.vm[:, l, :]
        update = m1 / (1.0 - beta_one**STEP) / (jnp.sqrt(m2 / (1.0 - beta_two**STEP)) + epsilon)
        S.vg[:, l, :] = g
        S.v1[:, l, :] = m1
        S.v2[:, l, :] = m2
        S.vm[:, l, :] = w - learn_rate * (update + decay_rate * w)

    loads[3].wait()
    loads[4].wait()
    pend, flush = [], nothing
    for l in reversed(range(L)):
        groups = spread(pend, 2 * NI)
        S.VG[...] = jnp.zeros_like(S.VG)

        def backward(i, c):
            bwd_mlp(S, l, i)
            at_points(groups[0::2], i, flush)
            bwd_attention(S, l, i)
            at_points(groups[1::2], i, flush)
            return c

        lax.fori_loop(0, NI, backward, 0)
        if l + 1 < L:
            adam(l + 1)
            for peer in peers:
                pl.semaphore_signal(S.credit, inc=1, device_id=(peer,), device_id_type=pl.DeviceIdType.MESH)
        grads_mlp(S, l)
        grads_attention(S, l)
        if l + 1 < L:
            pl.semaphore_wait(S.credit, len(peers))
        recv = recv_of(l)
        pack_and_send(net, S, S.wg.at[l], RB, S.rsend.at[l], recv, nd, rows)
        pend, flush = scatter_events(net, S.wg.at[l], RB, S.rsend.at[l], recv)

    def fin(i, c):
        S.vdx[i] = S.DX[i, 0:SEQ, :]
        return c

    lax.fori_loop(0, NI, fin, 0)
    out_dx = pltpu.make_async_copy(S.vdx, dimg, S.lsem.at[2])
    out_dx.start()
    for event in pend:
        event()
    adam(0)
    outs = [
        pltpu.make_async_copy(S.vm, o_master, S.lsem.at[0]),
        pltpu.make_async_copy(S.vg, o_grad, S.lsem.at[5]),
        pltpu.make_async_copy(S.v1, o_one, S.lsem.at[3]),
        pltpu.make_async_copy(S.v2, o_two, S.lsem.at[4]),
    ]
    for out in outs:
        out.start()
    out_act.wait()
    out_dx.wait()
    for out in outs:
        out.wait()


NAMES = (
    ["Wq", "Wp", "Wu", "Wd", "V", "VG", "F", "X", "DX", "DO", "DM", "DA", "DQKV", "wgs"]
    + [name for name, _, _ in SAVED]
    + ["rb0", "rb1a", "rb1b", "rb2a", "rb2b", "rb3a", "rb3b"]
    + ["vm", "v1", "v2", "vg", "vimg", "vcot", "vdx"]
    + ["lsem", "gsend", "grecv", "rsend", "rr0", "rr1", "rr2", "rr3", "credit"]
)


def body(topo, images, cotangent, counts, master, moment_one, moment_two):
    micro, slots = images.shape[:2]
    NI = micro * slots
    L, width = master.shape
    rows = width // 128
    RP = 16 * ((rows + 15) // 16)
    nd = lax.axis_size("fsdp")
    (nz, _), (n1, _), (n2, _), (nc, _) = topo
    cut = halves(RP)

    def rows_of(v):
        return v.reshape(L, rows, 128).transpose(1, 0, 2)

    def back(v):
        return v.transpose(1, 0, 2).reshape(L, width)

    VM, DMA = pltpu.VMEM, pltpu.SemaphoreType.DMA
    scratch = [
        VM((L, D, 3 * D), bf),
        VM((L, D, D), bf),
        VM((L, D, FF), bf),
        VM((L, FF, D), bf),
        VM((L, 16, FF), f32),
        VM((16, FF), f32),
        VM((nd * rows, 128), f32),
        VM((NI, TP, D), f32),
        VM((NI, TP, D), f32),
        VM((QP, D), bf),
        VM((NI, TP, D), bf),
        VM((NI, TP, D), bf),
        VM((NI, TP, 3 * D), bf),
        VM((L, nd, RP, 128), bf),
    ]
    scratch += [VM((L, NI) + shape, kind) for _, shape, kind in SAVED]
    scratch += [VM((max(nc - 1, 1), nz * n1 * n2, RP, 128), bf)]
    scratch += [
        VM((n2 - 1, nz * n1, cut[0][1], 128), bf),
        VM((n1 - 1, nz * n2, cut[1][1], 128), bf),
        VM((n1 - 1, nz, cut[0][1], 128), bf),
        VM((n2 - 1, nz, cut[1][1], 128), bf),
        VM((nz - 1, cut[0][1], 128), bf),
        VM((nz - 1, cut[1][1], 128), bf),
    ]
    scratch += [VM((rows, L, 128), f32)] * 4
    scratch += [VM((NI, SEQ, D), bf), VM((NI, SEQ, D), bf), VM((NI, SEQ, D), f32)]
    wide_first = max(n1, n2) - 1
    scratch += [
        DMA((6,)),
        DMA((L,)),
        DMA((L, 2, nd)),
        DMA((L,)),
        DMA((L, max(nc - 1, 1), nz * n1 * n2)),
        DMA((L, 2, wide_first, nz * max(n1, n2))),
        DMA((L, 2, wide_first, nz)),
        DMA((L, 2, nz - 1)),
        pltpu.SemaphoreType.REGULAR,
    ]
    anywhere = pl.BlockSpec(memory_space=pl.ANY)
    state = jax.ShapeDtypeStruct((rows, L, 128), f32)
    shape = (NI, SEQ, D)
    out = pl.pallas_call(
        functools.partial(kernel, (topo, L, NI, nd, rows, slots)),
        out_shape=(jax.ShapeDtypeStruct(shape, bf), jax.ShapeDtypeStruct(shape, f32), state, state, state, state),
        in_specs=[pl.BlockSpec(memory_space=pltpu.SMEM)] + [anywhere] * 5,
        out_specs=(anywhere,) * 6,
        scratch_shapes=scratch,
        compiler_params=pltpu.CompilerParams(vmem_limit_bytes=67043328, collective_id=0, has_side_effects=True),
        name="step",
    )(
        counts,
        images.reshape(shape),
        cotangent.reshape(shape),
        rows_of(master),
        rows_of(moment_one),
        rows_of(moment_two),
    )
    return (
        out[0].reshape(images.shape),
        out[1].reshape(images.shape),
        back(out[2]),
        back(out[3]),
        back(out[4]),
        back(out[5]),
    )


def solution(mesh):
    topo = topology(mesh)
    tokens = P(None, "fsdp", None, None)
    state = P(None, "fsdp")
    return jax.shard_map(
        functools.partial(body, topo),
        mesh=mesh,
        in_specs=(tokens, tokens, state, state, state, state),
        out_specs=(tokens, tokens, state, state, state, state),
        check_vma=False,
    )
```

profile of v0, /device:TPU:0, one launch (start us, length us, event | category | flops | bytes accessed | tf_op | source)
XLA Modules:
  0.0 161.8 jit_solution(8624870301810732354)
XLA Ops:
  0.6 0.0 copy-start.1
  0.6 1.4 copy.14.counts
  2.0 2.0 %copy.12 = bf16[2,2,197,384]{3,2,1,0:T(8,128)(2,1)} copy(bf16[2,2,197,384]{3,1,2,0:T(2,128)(2,1)} %param.6) | data formatting | bytes 1210368 | tf_op args[0]
  4.0 0.0 copy-done.1
  4.0 0.9 copy.13
  4.9 149.7 %step.1 = (bf16[4,197,384]{2,1,0:T(8,128)(2,1)}, f32[4,197,384]{2,1,0:T(8,128)}, f32[434,2,128]{2,1,0:T(2,128)}, f32[434,2,128]{2,1,0:T(2,128)}, f32[434,2,128]{2,1,0:T(2,128)}, /*index=5*/f32[434,2,128]{2,1,0:T(2,128)}) custom-call(s32[2,1]{1,0:T(2,128)} %copy.14.counts, bf16[4,197,384]{2,1,0:T(8,128)(2,1)} %bitcast.25, bf16[4,197,384]{2,1,0:T(8,128)(2,1)} %bitcast.26, ...), custom_call_target="tpu_custom_call" | custom-call | tf_op jit(solution)/shard_map/step/pallas_call | solution.py:760
  154.6 0.0 copy-start
  154.6 2.5 %copy.15 = bf16[2,2,197,384]{3,1,2,0:T(2,128)(2,1)} copy(bf16[2,2,197,384]{3,2,1,0:T(8,128)(2,1)} %bitcast.28) | data formatting | bytes 1210368
  157.1 0.0 copy-start.5
  157.1 0.0 copy-done
  157.1 0.0 copy-start.4
  157.1 1.6 %copy.16 = f32[2,2,197,384]{3,1,2,0:T(2,128)} copy(f32[2,2,197,384]{3,2,1,0:T(8,128)S(1)} %bitcast.27) | data formatting | bytes 2420736
  158.8 0.0 copy-done.5
  158.8 0.0 copy-start.3
  158.8 0.0 copy-start.2
  158.8 0.8 copy.21
  159.5 0.0 copy-done.4
  159.5 0.8 copy.22
  160.3 0.0 copy-done.3
  160.3 0.8 copy.23
  161.1 0.0 copy-done.2
  161.1 0.8 copy.24
Async XLA Ops:
  0.6 3.3 %copy-start.1 = (bf16[2,2,197,384]{3,1,2,0:T(2,128)(2,1)S(1)}, bf16[2,2,197,384]{3,1,2,0:T(2,128)(2,1)}, u32[]{:S(2)}) copy-start(bf16[2,2,197,384]{3,1,2,0:T(2,128)(2,1)} %param.7) | copy-start | bytes 1815556
  154.6 2.5 %copy-start = (f32[4,197,384]{2,1,0:T(8,128)S(1)}, f32[4,197,384]{2,1,0:T(8,128)}, u32[]{:S(2)}) copy-start(f32[4,197,384]{2,1,0:T(8,128)} %get-tuple-element.13) | copy-start | bytes 3631108
  157.1 1.7 %copy-start.5 = (f32[434,2,128]{2,1,0:T(2,128)S(1)}, f32[434,2,128]{2,1,0:T(2,128)}, u32[]{:S(2)}) copy-start(f32[434,2,128]{2,1,0:T(2,128)} %get-tuple-element.14) | copy-start | bytes 1333252
  157.1 2.4 %copy-start.4 = (f32[434,2,128]{2,1,0:T(2,128)S(1)}, f32[434,2,128]{2,1,0:T(2,128)}, u32[]{:S(2)}) copy-start(f32[434,2,128]{2,1,0:T(2,128)} %get-tuple-element.15) | copy-start | bytes 1333252
  158.8 1.5 copy-start.3
  158.8 2.3 %copy-start.2 = (f32[434,2,128]{2,1,0:T(2,128)S(1)}, f32[434,2,128]{2,1,0:T(2,128)}, u32[]{:S(2)}) copy-start(f32[434,2,128]{2,1,0:T(2,128)} %get-tuple-element.17) | copy-start | bytes 1333252
where the time goes:
time: 162 us
  Pallas kernels  150 us (93%)
  local copies, waits for them, and re-layouts  11.4 us (7%)
    pallas_call x1, Pallas kernels, body(): pl.pallas_call(functools.partial(kernel, (topo, L, NI, nd, rows, slots)),...  150 us
    unnamed x21, local copies, waits for them, and re-layouts  11.4 us

commit v1 on v0

--- a/solution.py
+++ b/solution.py
@@ -270,10 +270,18 @@
         self.at = [lax.rem(lax.div(self.me, stride), size) for size, stride in topo]
 
     def move(self, index, axis, by):
-        size, stride = self.topo[axis]
-        if by == 0 or size == 1:
+        if by == 0 or self.topo[axis][0] == 1:
             return index
-        return index + (lax.rem(self.at[axis] + by, size) - self.at[axis]) * stride
+        return index + (self.partner(axis, by) - self.at[axis]) * self.topo[axis][1]
+
+    def partner(self, axis, by):
+        at, out, weight, size = self.at[axis], 0, 1, self.topo[axis][0]
+        assert size & (size - 1) == 0
+        while weight < size:
+            bit = lax.rem(lax.div(at, weight), 2)
+            out = out + weight * (1 - bit if by & weight else bit)
+            weight *= 2
+        return out
 
     def block(self, offsets):
         index = self.me
@@ -299,65 +307,66 @@
     return ((0, first), (first, RP - first))
 
 
-def gather_events(net, wg, send, recv):
+def gather_plan(net, wg, send, recv):
     RP = wg.shape[1]
     cut = halves(RP)
     nz, n1, n2, nc = [size for size, _ in net.topo]
     orders = ((1, 2), (2, 1))
+    plan = NS()
 
     def copy(c, blk, peer):
         first, count = cut[c]
         ref = wg.at[blk, pl.ds(first, count), :]
         return remote(ref, ref, send, recv.at[c, blk], peer)
 
-    def targets(axes):
-        return [net.move(net.me, axis, by) for axis in axes for by in range(1, net.topo[axis][0])]
-
-    def forward(c, blk, axes):
-        for peer in targets(axes):
-            copy(c, blk, peer).start()
-
-    def arrived(c, blk, axes):
-        ends = targets(axes)
+    def wait(c, blk):
+        return lambda: copy(c, blk, net.me).wait_recv()
+
+    def give(c, blk, axis):
+        ends = [net.move(net.me, axis, by) for by in range(1, net.topo[axis][0])]
 
         def run():
-            copy(c, blk, net.me).wait_recv()
             for peer in ends:
                 copy(c, blk, peer).start()
 
         return run
 
-    events = []
-
-    def start():
+    def every(*steps):
+        def run():
+            for step in steps:
+                step()
+
+        return run
+
+    plan.along = every(*[every(*[
+        (lambda c=c, peer=peer: copy(c, net.me, peer).start()) for c in range(2)]) for peer in [net.move(net.me, 0, by) for by in range(1, nz)]])
+    plan.land, plan.near, plan.far, plan.core = [], [], [], []
+    plan.second, plan.third, plan.corner = [], [], []
+    for k in range(nz):
+        blk = net.block({0: k})
+        plan.land.append(every(*[wait(c, blk) for c in range(2)]) if k else every())
+        plan.near.append(every(*[give(c, blk, orders[c][0]) for c in range(2)]))
+        plan.far.append(every(*[give(c, blk, orders[c][1]) for c in range(2)]))
+        plan.core.append(every(*[give(c, blk, 3) for c in range(2)]))
+        second, third, corner = [], [], []
         for c in range(2):
-            forward(c, net.me, (0,))
-        for c in range(2):
-            forward(c, net.me, orders[c])
-        for c in range(2):
-            forward(c, net.me, (3,))
-
-    events.append((-1.0, start))
-    for c in range(2):
-        P, Q = orders[c]
-        sp, sq = net.topo[P][0], net.topo[Q][0]
-        for k in range(nz):
-            if k:
-                events.append((k, arrived(c, net.block({0: k}), (P, Q, 3))))
-            for jp in range(1, sp):
-                events.append((k + 1.1, arrived(c, net.block({0: k, P: jp}), (Q, 3))))
-            for jq in range(1, sq):
-                events.append((k + 1.2, arrived(c, net.block({0: k, Q: jq}), (3,))))
-                for jp in range(1, sp):
-                    events.append((k + 2.3, arrived(c, net.block({0: k, P: jp, Q: jq}), (3,))))
-        for k in range(nz):
-            for a in range(n1):
-                for b in range(n2):
-                    for w in range(1, nc):
-                        blk = net.block({0: k, 1: a, 2: b, 3: w})
-                        events.append((99.0, arrived(c, blk, ())))
-    events.sort(key=lambda e: e[0])
-    return [e[1] for e in events]
+            P, Q = orders[c]
+            for jp in range(1, net.topo[P][0]):
+                blk = net.block({0: k, P: jp})
+                second += [wait(c, blk), give(c, blk, Q), give(c, blk, 3)]
+                for jq in range(1, net.topo[Q][0]):
+                    blk = net.block({0: k, P: jp, Q: jq})
+                    corner += [wait(c, blk), give(c, blk, 3)]
+            for jq in range(1, net.topo[Q][0]):
+                blk = net.block({0: k, Q: jq})
+                third += [wait(c, blk), give(c, blk, 3)]
+        plan.second.append(every(*second))
+        plan.third.append(every(*third))
+        plan.corner.append(every(*corner))
+    plan.rest = every(*[
+        wait(c, net.block({0: k, 1: a, 2: b, 3: w}))
+        for k in range(nz) for a in range(n1) for b in range(n2) for w in range(1, nc) for c in range(2)])
+    return plan
 
 
 def wait_sends(buf, send, blocks):
@@ -384,7 +393,7 @@
         G[blk, rows(c), :] = G[blk, rows(c), :] + ref[...]
 
     def place(off, axis):
-        return lax.rem(net.at[axis] + off[axis], net.topo[axis][0])
+        return net.partner(axis, off[axis])
 
     def core_sum(off):
         blk = net.block(off)
@@ -528,13 +537,14 @@
                 flush()
 
 
-def kernel(cfg, counts, images, cotangent, master, one, two, act, dimg, o_grad, o_master, o_one, o_two, *scr):
+def kernel(cfg, counts, images, cotangent, master, act, dimg, o_grad, *scr):
     topo, L, NI, nd, rows, slots = cfg
     S = NS()
     for name, ref in zip(NAMES, scr):
         setattr(S, name, ref)
     S.wg = S.wgs
     net = Net(topo)
+    nz = topo[0][0]
 
     barrier = pltpu.get_barrier_semaphore()
     peers = net.peers()
@@ -545,8 +555,6 @@
         pltpu.make_async_copy(master, S.vm, S.lsem.at[0]),
         pltpu.make_async_copy(images, S.vimg, S.lsem.at[1]),
         pltpu.make_async_copy(cotangent, S.vcot, S.lsem.at[2]),
-        pltpu.make_async_copy(one, S.v1, S.lsem.at[3]),
-        pltpu.make_async_copy(two, S.v2, S.lsem.at[4]),
     ]
     for load in loads:
         load.start()
@@ -555,61 +563,87 @@
         S.wg[l, net.me, 0:rows, :] = S.vm[:, l, :].astype(bf)
     pl.semaphore_wait(barrier, len(peers))
 
-    gathers = [gather_events(net, S.wg.at[l], S.gsend.at[l], S.grecv.at[l]) for l in range(L)]
-    split = len(gathers[0])
-    gathers[0][0]()
-
-    def live(i):
-        return lax.rem(i, slots) < counts[lax.div(i, slots), 0]
+    gathers = [gather_plan(net, S.wg.at[l], S.gsend.at[l], S.grecv.at[l]) for l in range(L)]
+    now = gathers[0]
+    now.along()
+    now.near[0]()
+    now.far[0]()
+    now.core[0]()
+
+    def live(m, s):
+        return s < counts[0, m]
 
     loads[1].wait()
     loads[2].wait()
     edge = SEQ - SEQ % 16
 
-    def init(i, c):
-        S.X[i, edge:, :] = jnp.zeros((TP - edge, D), f32)
-        S.DX[i, edge:, :] = jnp.zeros((TP - edge, D), f32)
-        S.X[i, 0:SEQ, :] = S.vimg[i].astype(f32)
-        S.DX[i, 0:SEQ, :] = jnp.where(live(i), S.vcot[i].astype(f32), 0.0)
-        for l in range(L):
-            S.Q[l, i, TP:, :] = jnp.zeros((QP - TP, D), bf)
+    def init(m, c):
+        S.vdx[m] = S.vimg[m].astype(f32)
+        for s in range(slots):
+            i = m * slots + s
+            S.X[i, edge:, :] = jnp.zeros((TP - edge, D), f32)
+            S.DX[i, edge:, :] = jnp.zeros((TP - edge, D), f32)
+            S.X[i, 0:SEQ, :] = S.vdx[m, :, s, :]
+            for l in range(L):
+                S.Q[l, i, TP:, :] = jnp.zeros((QP - TP, D), bf)
+        S.vdx[m] = S.vcot[m].astype(f32)
+        for s in range(slots):
+            S.DX[m * slots + s, 0:SEQ, :] = jnp.where(live(m, s), S.vdx[m, :, s, :], 0.0)
         return c
 
-    lax.fori_loop(0, NI, init, 0)
+    lax.fori_loop(0, NI // slots, init, 0)
     S.DO[TP:, :] = jnp.zeros((QP - TP, D), bf)
 
-    for event in gathers[0][1:]:
-        event()
+    steps = []
+    for k in range(nz):
+        at = 3.4 * k
+        if k:
+            steps += [(at, now.land[k]), (at, now.near[k]), (at, now.far[k]), (at, now.core[k])]
+        steps += [(at + 3.3, now.second[k]), (at + 4.5, now.third[k]), (at + 7.5, now.corner[k])]
+    steps.append((3.4 * (nz - 1) + 0.1, lambda: [g.along() for g in gathers[1:2]]))
+    steps.append((3.4 * (nz - 1) + 3.4, lambda: [part() for g in gathers[1:2] for part in (g.near[0], g.far[0], g.core[0])]))
+    for _, step in sorted(steps, key=lambda e: e[0]):
+        step()
+    now.rest()
     unpack_layer(S, 0, nd, rows)
 
     def nothing():
         pass
 
-    flush = nothing
     for l in range(L):
-        groups = []
+        groups = [[] for _ in range(2 * NI)]
         if l + 1 < L:
-            gathers[l + 1][0]()
-            groups = spread(gathers[l + 1][1:], 2 * NI)
+            g = gathers[l + 1]
+            if l:
+                g.along()
+                g.near[0]()
+                g.far[0]()
+                g.core[0]()
+            for k in range(1, nz):
+                g.land[k]()
+                g.near[k]()
+            for part in (g.far, g.core):
+                for k in range(1, nz):
+                    part[k]()
+            g.second[0]()
+            late = [(1.6 + 1.4 * k, g.second[k]) for k in range(1, nz)]
+            late += [(4.8 + 1.4 * k, g.third[k]) for k in range(nz)]
+            late += [(9.8 + 1.4 * k, g.corner[k]) for k in range(nz)]
+            for at, step in sorted(late, key=lambda e: e[0]):
+                groups[min(max(int(at / 1.6) - 1, 0), 2 * NI - 1)].append(step)
 
         def forward(i, c):
             fwd_attention(S, l, i)
-            at_points(groups[0::2], i, flush)
+            at_points(groups[0::2], i, nothing)
             fwd_mlp(S, l, i)
-            at_points(groups[1::2], i, flush)
+            at_points(groups[1::2], i, nothing)
             return c
 
         lax.fori_loop(0, NI, forward, 0)
         if l + 1 < L:
+            g.rest()
             unpack_layer(S, l + 1, nd, rows)
 
-    def finish(i, c):
-        S.vimg[i] = jnp.where(live(i), S.X[i, 0:SEQ, :], 0.0).astype(bf)
-        return c
-
-    lax.fori_loop(0, NI, finish, 0)
-    out_act = pltpu.make_async_copy(S.vimg, act, S.lsem.at[1])
-    out_act.start()
     for l in range(L):
         wait_sends(S.wg.at[l], S.gsend.at[l], nd - 1)
 
@@ -619,29 +653,19 @@
     def recv_of(l):
         return [S.rr0.at[l], [S.rr1.at[l, c] for c in range(2)], [S.rr2.at[l, c] for c in range(2)], [S.rr3.at[l, c] for c in range(2)]]
 
-    def adam(l):
+    def total(l):
         wait_sends(S.wg.at[l], S.rsend.at[l], nd - 1)
         g = []
         for c, (first, count) in enumerate(halves(S.wg.shape[2])):
             part = S.wg[l, net.me, pl.ds(first, count), :].astype(f32)
-            for by in range(topo[0][0] - 1):
+            for by in range(nz - 1):
                 part = part + RB[3][c][by].astype(f32)
             g.append(part)
-        g = jnp.concatenate(g, axis=0)[0:rows] * (1.0 / (NI * nd))
-        m1 = beta_one * S.v1[:, l, :] + (1.0 - beta_one) * g
-        m2 = beta_two * S.v2[:, l, :] + (1.0 - beta_two) * g * g
-        w = S.vm[:, l, :]
-        update = m1 / (1.0 - beta_one**STEP) / (jnp.sqrt(m2 / (1.0 - beta_two**STEP)) + epsilon)
-        S.vg[:, l, :] = g
-        S.v1[:, l, :] = m1
-        S.v2[:, l, :] = m2
-        S.vm[:, l, :] = w - learn_rate * (update + decay_rate * w)
-
-    loads[3].wait()
-    loads[4].wait()
+        S.vm[:, l, :] = jnp.concatenate(g, axis=0)[0:rows]
+
     pend, flush = [], nothing
     for l in reversed(range(L)):
-        groups = spread(pend, 2 * NI)
+        groups = spread(pend[:-1], 2 * NI)
         S.VG[...] = jnp.zeros_like(S.VG)
 
         def backward(i, c):
@@ -652,38 +676,35 @@
             return c
 
         lax.fori_loop(0, NI, backward, 0)
-        if l + 1 < L:
-            adam(l + 1)
-            for peer in peers:
-                pl.semaphore_signal(S.credit, inc=1, device_id=(peer,), device_id_type=pl.DeviceIdType.MESH)
         grads_mlp(S, l)
         grads_attention(S, l)
         if l + 1 < L:
+            pend[-1]()
+            total(l + 1)
+            for peer in peers:
+                pl.semaphore_signal(S.credit, inc=1, device_id=(peer,), device_id_type=pl.DeviceIdType.MESH)
             pl.semaphore_wait(S.credit, len(peers))
         recv = recv_of(l)
         pack_and_send(net, S, S.wg.at[l], RB, S.rsend.at[l], recv, nd, rows)
         pend, flush = scatter_events(net, S.wg.at[l], RB, S.rsend.at[l], recv)
 
-    def fin(i, c):
-        S.vdx[i] = S.DX[i, 0:SEQ, :]
+    def out_tokens(m, c):
+        for s in range(slots):
+            S.vdx[m, :, s, :] = jnp.where(live(m, s), S.X[m * slots + s, 0:SEQ, :], 0.0)
+        S.vimg[m] = S.vdx[m].astype(bf)
+        for s in range(slots):
+            S.vdx[m, :, s, :] = S.DX[m * slots + s, 0:SEQ, :]
         return c
 
-    lax.fori_loop(0, NI, fin, 0)
-    out_dx = pltpu.make_async_copy(S.vdx, dimg, S.lsem.at[2])
-    out_dx.start()
+    lax.fori_loop(0, NI // slots, out_tokens, 0)
+    outs = [pltpu.make_async_copy(S.vimg, act, S.lsem.at[1]), pltpu.make_async_copy(S.vdx, dimg, S.lsem.at[2])]
+    for out in outs:
+        out.start()
     for event in pend:
         event()
-    adam(0)
-    outs = [
-        pltpu.make_async_copy(S.vm, o_master, S.lsem.at[0]),
-        pltpu.make_async_copy(S.vg, o_grad, S.lsem.at[5]),
-        pltpu.make_async_copy(S.v1, o_one, S.lsem.at[3]),
-        pltpu.make_async_copy(S.v2, o_two, S.lsem.at[4]),
-    ]
-    for out in outs:
-        out.start()
-    out_act.wait()
-    out_dx.wait()
+    total(0)
+    outs.append(pltpu.make_async_copy(S.vm, o_grad, S.lsem.at[0]))
+    outs[-1].start()
     for out in outs:
         out.wait()
 
@@ -692,7 +713,7 @@
     ["Wq", "Wp", "Wu", "Wd", "V", "VG", "F", "X", "DX", "DO", "DM", "DA", "DQKV", "wgs"]
     + [name for name, _, _ in SAVED]
     + ["rb0", "rb1a", "rb1b", "rb2a", "rb2b", "rb3a", "rb3b"]
-    + ["vm", "v1", "v2", "vg", "vimg", "vcot", "vdx"]
+    + ["vm", "vimg", "vcot", "vdx"]
     + ["lsem", "gsend", "grecv", "rsend", "rr0", "rr1", "rr2", "rr3", "credit"]
 )
 
@@ -706,12 +727,6 @@
     nd = lax.axis_size("fsdp")
     (nz, _), (n1, _), (n2, _), (nc, _) = topo
     cut = halves(RP)
-
-    def rows_of(v):
-        return v.reshape(L, rows, 128).transpose(1, 0, 2)
-
-    def back(v):
-        return v.transpose(1, 0, 2).reshape(L, width)
 
     VM, DMA = pltpu.VMEM, pltpu.SemaphoreType.DMA
     scratch = [
@@ -740,11 +755,11 @@
         VM((nz - 1, cut[0][1], 128), bf),
         VM((nz - 1, cut[1][1], 128), bf),
     ]
-    scratch += [VM((rows, L, 128), f32)] * 4
-    scratch += [VM((NI, SEQ, D), bf), VM((NI, SEQ, D), bf), VM((NI, SEQ, D), f32)]
+    tokens = (micro, SEQ, slots, D)
+    scratch += [VM((rows, L, 128), f32), VM(tokens, bf), VM(tokens, bf), VM(tokens, f32)]
     wide_first = max(n1, n2) - 1
     scratch += [
-        DMA((6,)),
+        DMA((3,)),
         DMA((L,)),
         DMA((L, 2, nd)),
         DMA((L,)),
@@ -755,31 +770,36 @@
         pltpu.SemaphoreType.REGULAR,
     ]
     anywhere = pl.BlockSpec(memory_space=pl.ANY)
-    state = jax.ShapeDtypeStruct((rows, L, 128), f32)
-    shape = (NI, SEQ, D)
-    out = pl.pallas_call(
+    act, grad_in, grad = pl.pallas_call(
         functools.partial(kernel, (topo, L, NI, nd, rows, slots)),
-        out_shape=(jax.ShapeDtypeStruct(shape, bf), jax.ShapeDtypeStruct(shape, f32), state, state, state, state),
-        in_specs=[pl.BlockSpec(memory_space=pltpu.SMEM)] + [anywhere] * 5,
-        out_specs=(anywhere,) * 6,
+        out_shape=(
+            jax.ShapeDtypeStruct(tokens, bf),
+            jax.ShapeDtypeStruct(tokens, f32),
+            jax.ShapeDtypeStruct((rows, L, 128), f32),
+        ),
+        in_specs=[pl.BlockSpec(memory_space=pltpu.SMEM)] + [anywhere] * 3,
+        out_specs=(anywhere,) * 3,
         scratch_shapes=scratch,
         compiler_params=pltpu.CompilerParams(vmem_limit_bytes=67043328, collective_id=0, has_side_effects=True),
         name="step",
     )(
-        counts,
-        images.reshape(shape),
-        cotangent.reshape(shape),
-        rows_of(master),
-        rows_of(moment_one),
-        rows_of(moment_two),
+        counts.T,
+        images.transpose(0, 2, 1, 3),
+        cotangent.transpose(0, 2, 1, 3),
+        master.reshape(L, rows, 128).transpose(1, 0, 2),
     )
+    weight_grad = grad.transpose(1, 0, 2).reshape(L, width) / (NI * nd)
+    first_new = beta_one * moment_one + (1.0 - beta_one) * weight_grad
+    second_new = beta_two * moment_two + (1.0 - beta_two) * weight_grad * weight_grad
+    update = first_new / (1.0 - beta_one**STEP) / (jnp.sqrt(second_new / (1.0 - beta_two**STEP)) + epsilon)
+    new_master = master - learn_rate * (update + decay_rate * master)
     return (
-        out[0].reshape(images.shape),
-        out[1].reshape(images.shape),
-        back(out[2]),
-        back(out[3]),
-        back(out[4]),
-        back(out[5]),
+        act.transpose(0, 2, 1, 3),
+        grad_in.transpose(0, 2, 1, 3),
+        weight_grad,
+        new_master,
+        first_new,
+        second_new,
     )
 
 

time: 162 us -> 140 us (0.86)
  Pallas kernels: 150 us -> 133 us
  local copies, waits for them, and re-layouts: 11.4 us -> 2.52 us
  other arithmetic: 0 us -> 4.21 us
    pallas_call x1, Pallas kernels: 150 us -> 133 us  [body(): pl.pallas_call(functools.partial(kernel, (topo, L, NI, nd, rows, slots)),...]
    unnamed x21 -> x6, local copies, waits for them, and re-layouts: 11.4 us -> 2.52 us
    sub x0 -> x1, other arithmetic: none -> 4.21 us  [body(): new_master = master - learn_rate * (update + decay_rate * master)]
where the time goes in v1:
time: 140 us
  Pallas kernels  133 us (95%)
  other arithmetic  4.21 us (3%)
  local copies, waits for them, and re-layouts  2.52 us (2%)
    pallas_call x1, Pallas kernels, body(): pl.pallas_call(functools.partial(kernel, (topo, L, NI, nd, rows, slots)),...  133 us
    sub x1, other arithmetic, body(): new_master = master - learn_rate * (update + decay_rate * master)  4.21 us

profile of v1, /device:TPU:0, one launch (start us, length us, event | category | flops | bytes accessed | tf_op | source)
XLA Modules:
  0.0 140.0 jit_solution(11694723559941967339)
XLA Ops:
  0.6 132.6 %step.1 = (bf16[2,197,2,384]{3,2,1,0:T(2,128)(2,1)}, f32[2,197,2,384]{3,2,1,0:T(2,128)}, f32[434,2,128]{2,1,0:T(2,128)}) custom-call(s32[1,2]{1,0:T(1,128)} %bitcast.30, bf16[2,197,2,384]{3,2,1,0:T(2,128)(2,1)} %bitcast.27, bf16[2,197,2,384]{3,2,1,0:T(2,128)(2,1)} %bitcast.28, f32[434,2,128]{2,1,0:T(2,128)} %bitcast.25), custom_call_target="tpu_custom_call" | custom-call | tf_op jit(solution)/shard_map/step/pallas_call | solution.py:773
  133.3 0.0 copy-start.1
  133.3 4.2 %multiply_subtract_fusion = (f32[2,55552]{1,0:T(2,128)}, f32[2,55552]{1,0:T(2,128)}, f32[2,55552]{1,0:T(2,128)}, f32[2,55552]{1,0:T(2,128)}) fusion(f32[2,55552]{1,0:T(2,128)} %param.9, f32[434,2,128]{2,1,0:T(2,128)} %get-tuple-element.11, f32[2,55552]{1,0:T(2,128)} %param.10, f32[2,55552]{1,0:T(2,128)} %param.11), kind=kLoop, calls=%fused_computation.3 | loop fusion | flops 1777664 | bytes 3555328 | tf_op jit(solution)/shard_map/sub | solution.py:795
  137.5 0.0 copy-start
  137.5 0.0 copy-done.1
  137.5 0.8 copy.14
  138.3 0.7 copy-done
  139.0 1.0 copy.15
Async XLA Ops:
  133.3 4.2 %copy-start.1 = (bf16[2,197,2,384]{3,2,1,0:T(2,128)(2,1)S(1)}, bf16[2,197,2,384]{3,2,1,0:T(2,128)(2,1)}, u32[]{:S(2)}) copy-start(bf16[2,197,2,384]{3,2,1,0:T(2,128)(2,1)} %get-tuple-element.9) | copy-start | bytes 1815556
  137.5 1.5 %copy-start = (f32[2,197,2,384]{3,2,1,0:T(2,128)S(1)}, f32[2,197,2,384]{3,2,1,0:T(2,128)}, u32[]{:S(2)}) copy-start(f32[2,197,2,384]{3,2,1,0:T(2,128)} %get-tuple-element.10) | copy-start | bytes 3631108

commit v2 on v1

--- a/solution.py
+++ b/solution.py
@@ -217,21 +217,28 @@
         F[pl.ds(first + j, val.shape[0], stride=n), :] = val[:, 128 * j : 128 * j + 128]
 
 
-def grads_mlp(S, l):
-    V, F = S.V, S.F
+def grads_down(S, l):
+    F = S.F
     dm = flat(S.DM[...])
     for c in range(3):
         gb = flat(S.GB[l, :, :, 512 * c : 512 * c + 512])
         store_grad(F, dot(gb, dm, TN), R_D + 3 * 512 * c, 3)
+
+
+def grads_up(S, l):
+    V, F = S.V, S.F
     h2 = (flat(S.N2[l]).astype(f32) * V[l, G2 : G2 + 1, 0:D] + V[l, B2 : B2 + 1, 0:D]).astype(bf)
     for c in range(3):
         du = flat(S.GP[l, :, :, 512 * c : 512 * c + 512])
         store_grad(F, dot(h2, du, TN), R_U + 4 * c, 12)
 
 
+def grads_out(S, l):
+    store_grad(S.F, dot(flat(S.O[l]), flat(S.DA[...]), TN), R_P, 3)
+
+
 def grads_attention(S, l):
     V, VG, F = S.V, S.VG, S.F
-    store_grad(F, dot(flat(S.O[l]), flat(S.DA[...]), TN), R_P, 3)
     h = (flat(S.N1[l]).astype(f32) * V[l, G1 : G1 + 1, 0:D] + V[l, B1 : B1 + 1, 0:D]).astype(bf)
     for c0, c1 in ((0, 512), (512, 1024), (1024, 1152)):
         store_grad(F, dot(h, flat(S.DQKV[:, :, c0:c1]), TN), R_QKV + c0 // 128, 9)
@@ -302,16 +309,20 @@
     )
 
 
-def halves(RP):
-    first = 16 * ((RP // 16 + 1) // 2)
-    return ((0, first), (first, RP - first))
+PARTS = 4
+
+
+def parts(RP):
+    tiles = RP // 16
+    ends = [16 * (tiles * p // PARTS) for p in range(PARTS + 1)]
+    return [(ends[p], ends[p + 1] - ends[p]) for p in range(PARTS)]
 
 
 def gather_plan(net, wg, send, recv):
     RP = wg.shape[1]
-    cut = halves(RP)
+    cut = parts(RP)
     nz, n1, n2, nc = [size for size, _ in net.topo]
-    orders = ((1, 2), (2, 1))
+    orders = ((1, 2), (2, 1)) * (PARTS // 2)
     plan = NS()
 
     def copy(c, blk, peer):
@@ -339,17 +350,17 @@
         return run
 
     plan.along = every(*[every(*[
-        (lambda c=c, peer=peer: copy(c, net.me, peer).start()) for c in range(2)]) for peer in [net.move(net.me, 0, by) for by in range(1, nz)]])
+        (lambda c=c, peer=peer: copy(c, net.me, peer).start()) for c in range(PARTS)]) for peer in [net.move(net.me, 0, by) for by in range(1, nz)]])
     plan.land, plan.near, plan.far, plan.core = [], [], [], []
     plan.second, plan.third, plan.corner = [], [], []
     for k in range(nz):
         blk = net.block({0: k})
-        plan.land.append(every(*[wait(c, blk) for c in range(2)]) if k else every())
-        plan.near.append(every(*[give(c, blk, orders[c][0]) for c in range(2)]))
-        plan.far.append(every(*[give(c, blk, orders[c][1]) for c in range(2)]))
-        plan.core.append(every(*[give(c, blk, 3) for c in range(2)]))
+        plan.land.append(every(*[wait(c, blk) for c in range(PARTS)]) if k else every())
+        plan.near.append(every(*[give(c, blk, orders[c][0]) for c in range(PARTS)]))
+        plan.far.append(every(*[give(c, blk, orders[c][1]) for c in range(PARTS)]))
+        plan.core.append(every(*[give(c, blk, 3) for c in range(PARTS)]))
         second, third, corner = [], [], []
-        for c in range(2):
+        for c in range(PARTS):
             P, Q = orders[c]
             for jp in range(1, net.topo[P][0]):
                 blk = net.block({0: k, P: jp})
@@ -365,7 +376,7 @@
         plan.corner.append(every(*corner))
     plan.rest = every(*[
         wait(c, net.block({0: k, 1: a, 2: b, 3: w}))
-        for k in range(nz) for a in range(n1) for b in range(n2) for w in range(1, nc) for c in range(2)])
+        for k in range(nz) for a in range(n1) for b in range(n2) for w in range(1, nc) for c in range(PARTS)])
     return plan
 
 
@@ -374,17 +385,39 @@
     pltpu.make_async_copy(ref, ref, send).wait()
 
 
-def scatter_events(net, G, RB, send, recv):
+def run(events):
+    def when(test, do):
+        if do is None:
+            return
+        if test is None:
+            do()
+        else:
+            pl.when(test)(do)
+
+    previous = None
+    for *_, take, take_if, give, give_if in events:
+        when(take_if, take)
+        if previous is not None:
+            when(*previous)
+        previous = (give_if, give)
+    if previous is not None:
+        when(*previous)
+
+
+def both(*tests):
+    out = None
+    for test in tests:
+        if test is not None:
+            out = test if out is None else jnp.logical_and(out, test)
+    return out
+
+
+def scatter_plan(net, G, RB, send, recv, bounds, margin):
     RP = G.shape[1]
-    cut = halves(RP)
+    cut = parts(RP)
     nz, n1, n2, nc = [size for size, _ in net.topo]
-    orders = ((2, 1), (1, 2))
-    pending = []
-
-    def flush():
-        for start in pending:
-            start()
-        del pending[:]
+    orders = ((2, 1), (1, 2)) * (PARTS // 2)
+    low = nz.bit_length() - 1
 
     def rows(c):
         return pl.ds(cut[c][0], cut[c][1])
@@ -392,149 +425,190 @@
     def add(ref, blk, c):
         G[blk, rows(c), :] = G[blk, rows(c), :] + ref[...]
 
-    def place(off, axis):
-        return net.partner(axis, off[axis])
-
-    def core_sum(off):
-        blk = net.block(off)
-        s = (place(off, 0) * n1 + place(off, 1)) * n2 + place(off, 2)
+    def bit(v, s):
+        return lax.rem(lax.div(v, 1 << s), 2)
+
+    def block(g, off):
+        blk = net.block({axis: by for axis, by in off.items()})
+        return blk + (g - net.at[0]) * net.topo[0][1]
+
+    def core_sum(g, off):
+        blk = block(g, off)
+        spot = (g * n1 + net.partner(1, off[1])) * n2 + net.partner(2, off[2])
         sends = []
-        for c in range(2):
+        for c in range(PARTS):
             Q, P = orders[c]
-            by = off[Q]
-            if by:
-                spot = place(off, 0) * net.topo[P][0] + place(off, P)
-                peer = net.move(net.me, Q, by)
-                sends.append((c, by - 1, spot, peer))
-
-        def run():
+            if off[Q]:
+                sends.append((c, off[Q] - 1, g * net.topo[P][0] + net.partner(P, off[P]), net.move(net.me, Q, off[Q])))
+
+        def take():
             for w in range(1, nc):
-                remote(RB[0].at[w - 1, s], RB[0].at[w - 1, s], send, recv[0].at[w - 1, s], net.me).wait_recv()
-            for c in range(2):
-                for w in range(1, nc):
-                    add(RB[0].at[w - 1, s, rows(c), :], blk, c)
-            flush()
-            for c, by, spot, peer in sends:
-                pending.append(lambda c=c, by=by, spot=spot, peer=peer: remote(
-                    G.at[blk, rows(c), :], RB[1][c].at[by, spot], send, recv[1][c].at[by, spot], peer).start())
-
-        return run
-
-    def second(c, off):
+                ref = RB[0].at[w - 1, spot]
+                remote(ref, ref, send, recv[0].at[w - 1, spot], net.me).wait_recv()
+            for w in range(1, nc):
+                for c in range(PARTS):
+                    add(RB[0].at[w - 1, spot, rows(c), :], blk, c)
+
+        def give():
+            for c, by, to, peer in sends:
+                remote(G.at[blk, rows(c), :], RB[1][c].at[by, to], send, recv[1][c].at[by, to], peer).start()
+
+        return take, None, give if sends else None, None
+
+    def second(c, g, off):
         Q, P = orders[c]
-        blk = net.block(off)
-        at_z = place(off, 0)
-        spot = at_z * net.topo[P][0] + place(off, P)
+        blk = block(g, off)
+        spot = g * net.topo[P][0] + net.partner(P, off[P])
         by = off[P]
         peer = net.move(net.me, P, by)
 
-        def run():
+        def take():
             for j in range(net.topo[Q][0] - 1):
                 ref = RB[1][c].at[j, spot]
                 remote(ref, ref, send, recv[1][c].at[j, spot], net.me).wait_recv()
                 add(ref, blk, c)
-            flush()
-            if by:
-                pending.append(lambda: remote(
-                    G.at[blk, rows(c), :], RB[2][c].at[by - 1, at_z], send, recv[2][c].at[by - 1, at_z], peer).start())
-
-        return run
-
-    def third(c, off):
+
+        def give():
+            remote(G.at[blk, rows(c), :], RB[2][c].at[by - 1, g], send, recv[2][c].at[by - 1, g], peer).start()
+
+        return take, None, give if by else None, None
+
+    def slot(g, s):
+        return sum(nz >> (t + 1) for t in range(s)) + (g >> (s + 1))
+
+    def along(c, g, s):
+        blk = block(g, {1: 0, 2: 0})
+        peer = net.move(net.me, 0, 1 << s)
+
+        def give():
+            at = slot(g, s)
+            remote(G.at[blk, rows(c), :], RB[3][c].at[at], send, recv[3][c].at[at], peer).start()
+
+        return give, (bit(net.at[0], s) != (g >> s) % 2)
+
+    def third(c, g):
         Q, P = orders[c]
-        blk = net.block(off)
-        at_z = place(off, 0)
-        by = off[0]
-        peer = net.move(net.me, 0, by)
-
-        def run():
+        blk = block(g, {1: 0, 2: 0})
+
+        def take():
             for j in range(net.topo[P][0] - 1):
-                ref = RB[2][c].at[j, at_z]
-                remote(ref, ref, send, recv[2][c].at[j, at_z], net.me).wait_recv()
+                ref = RB[2][c].at[j, g]
+                remote(ref, ref, send, recv[2][c].at[j, g], net.me).wait_recv()
                 add(ref, blk, c)
-            flush()
-            if by:
-                pending.append(lambda: remote(
-                    G.at[blk, rows(c), :], RB[3][c].at[by - 1], send, recv[3][c].at[by - 1], peer).start())
-
-        return run
-
-    def last():
-        flush()
-        for c in range(2):
-            for by in range(1, nz):
-                ref = RB[3][c].at[by - 1]
-                remote(ref, ref, send, recv[3][c].at[by - 1], net.me).wait_recv()
-
-    events = []
-    z_order = [k for k in range(1, nz)] + [0]
+
+        return (take, None) + (along(c, g, 0) if low else (None, None))
+
+    def halving(c, g, s):
+        blk = block(g, {1: 0, 2: 0})
+        same = lax.rem(net.at[0], 2 << s) == g % (2 << s)
+
+        def take():
+            at = slot(g, s)
+            ref = RB[3][c].at[at]
+            remote(ref, ref, send, recv[3][c].at[at], net.me).wait_recv()
+            add(ref, blk, c)
+
+        give, differs = along(c, g, s + 1)
+        return take, same, give, jnp.logical_and(same, differs)
+
+    def member(g, off, inside):
+        if len(inside) == n1 * n2:
+            return None
+        a, b = net.partner(1, off[1]), net.partner(2, off[2])
+        spot = a * n2 + b
+        return both(spot >= inside[0], spot <= inside[-1])
+
     plane = sorted(((a, b) for a in range(n1) for b in range(n2)), key=lambda ab: -((ab[0] > 0) + (ab[1] > 0)))
-    for r, k in enumerate(z_order):
-        for a, b in plane:
-            events.append((r, core_sum({0: k, 1: a, 2: b})))
-        for c in range(2):
-            Q, P = orders[c]
-            for j in list(range(1, net.topo[P][0])) + [0]:
-                events.append((r + 1.5 + 0.1 * (j == 0), second(c, {0: k, P: j, Q: 0})))
-            events.append((r + 2.7, third(c, {0: k, P: 0, Q: 0})))
-    events.sort(key=lambda e: e[0])
-    return [e[1] for e in events] + [last], flush
-
-
-def pack_and_send(net, S, G, RB, send, recv, nd, rows):
+    lists = []
+    for w in range(len(bounds) - 1):
+        events, n = [], 0
+        hidden = w + 2 < len(bounds) or margin > 1.0
+        slack = margin * hidden
+        for g in reversed(range(nz)):
+            inside = [t % (n1 * n2) for t in range(bounds[w + 1], bounds[w]) if t // (n1 * n2) == g]
+            if not inside:
+                continue
+
+            def put(at, stage, event, off):
+                take, take_if, give, give_if = event
+                test = member(g, off, inside)
+                events.append([at, stage, (id(G), w, g), take, both(test, take_if), give, both(test, give_if)])
+
+            for r, (a, b) in enumerate(plane):
+                put(1.2 + 0.5 * slack + 1.2 * n + 0.3 * r, 0, core_sum(g, {1: a, 2: b}), {1: a, 2: b})
+            for c in range(PARTS):
+                Q, P = orders[c]
+                for j in list(range(1, net.topo[P][0])) + [0]:
+                    off = {P: j, Q: 0}
+                    put(4.0 + slack + 2.6 * n + 1.3 * (j == 0) + 0.1 * c, 1 + (j == 0), second(c, g, off), off)
+                after = max(6.8 + 2.6 * n, (10.8 + 1.3 * n) * hidden) + slack + 0.1 * c
+                put(after, 3, third(c, g), {1: 0, 2: 0})
+                for s in range(low - 1):
+                    put(after + 2.5 * (s + 1) + (7.5 if margin > 1.0 else 4.0) * hidden, 4 + s, halving(c, g, s), {1: 0, 2: 0})
+            n += 1
+        lists.append(sorted(events, key=lambda e: e[0]))
+    return lists
+
+
+def pack_and_send(net, S, G, RB, send, recv, nd, rows, chips):
     nz, n1, n2, nc = [size for size, _ in net.topo]
     F = S.F
-
-    def chip(t):
-        a = lax.div(t, n1 * n2)
-        b = lax.rem(lax.div(t, n2), n1)
-        g = lax.rem(t, n2)
-        base = a * net.topo[0][1] + b * net.topo[1][1] + g * net.topo[2][1]
-        return base
+    first, last = chips
+
+    def block(t, w):
+        base = lax.div(t, n1 * n2) * net.topo[0][1] + lax.rem(lax.div(t, n2), n1) * net.topo[1][1] + lax.rem(t, n2) * net.topo[2][1]
+        core = net.at[3] if w == 0 else net.partner(3, w)
+        return base + core * net.topo[3][1]
 
     def pack(blk):
         G[blk, 0:rows, :] = F[pl.ds(rows * blk, rows), :].astype(bf)
 
     def go(t, w):
-        blk = chip(t) + lax.rem(net.at[3] + w, nc) * net.topo[3][1]
-        remote(G.at[blk], RB[0].at[w - 1, t], send, recv[0].at[w - 1, t], net.move(net.me, 3, w)).start()
-
-    total = nz * n1 * n2
+        remote(G.at[block(t, w)], RB[0].at[w - 1, t], send, recv[0].at[w - 1, t], net.move(net.me, 3, w)).start()
+
     for w in range(1, nc):
-        def step(t, c):
-            pack(chip(t) + lax.rem(net.at[3] + w, nc) * net.topo[3][1])
-
-            @pl.when(t > 0)
+
+        def step(k, c):
+            t = last - 1 - k
+            pack(block(t, w))
+
+            @pl.when(k > 0)
             def _():
-                go(t - 1, w)
+                go(t + 1, w)
 
             return c
 
-        lax.fori_loop(0, total, step, 0)
-
-    def mine(t, c):
-        pack(chip(t) + net.at[3] * net.topo[3][1])
+        lax.fori_loop(0, last - first, step, 0)
+
+    def mine(k, c):
+        pack(block(last - 1 - k, 0))
         return c
 
-    lax.fori_loop(0, total, mine, 0)
+    lax.fori_loop(0, last - first, mine, 0)
     for w in range(1, nc):
-        go(total - 1, w)
-
-
-def spread(events, points):
-    n = len(events)
-    return [events[n * p // points : n * (p + 1) // points] for p in range(points)]
-
-
-def at_points(groups, index, flush):
+        go(first, w)
+
+
+def chips_before(topo, rows, row):
+    (nz, sz), (n1, s1), (n2, s2), _ = topo
+    count = 0
+    for t in range(nz * n1 * n2):
+        base = (t // (n1 * n2)) * sz + (t // n2 % n1) * s1 + (t % n2) * s2
+        if rows * base < row:
+            count = t + 1
+    return count
+
+
+AFTER = [0.0, 2.4, 3.4, 4.8, 7.4] + [10.4 + 3.0 * k for k in range(8)]
+
+
+def at_points(groups, index):
     for value, group in enumerate(groups):
         if group:
 
             @pl.when(index == value)
             def _(group=group):
-                for event in group:
-                    event()
-                flush()
+                run(group)
 
 
 def kernel(cfg, counts, images, cotangent, master, act, dimg, o_grad, *scr):
@@ -606,9 +680,6 @@
         step()
     now.rest()
     unpack_layer(S, 0, nd, rows)
-
-    def nothing():
-        pass
 
     for l in range(L):
         groups = [[] for _ in range(2 * NI)]
@@ -630,13 +701,13 @@
             late += [(4.8 + 1.4 * k, g.third[k]) for k in range(nz)]
             late += [(9.8 + 1.4 * k, g.corner[k]) for k in range(nz)]
             for at, step in sorted(late, key=lambda e: e[0]):
-                groups[min(max(int(at / 1.6) - 1, 0), 2 * NI - 1)].append(step)
+                groups[min(max(int(at / 1.6) - 1, 0), 2 * NI - 1)].append((step, None, None, None))
 
         def forward(i, c):
             fwd_attention(S, l, i)
-            at_points(groups[0::2], i, nothing)
+            at_points(groups[0::2], i)
             fwd_mlp(S, l, i)
-            at_points(groups[1::2], i, nothing)
+            at_points(groups[1::2], i)
             return c
 
         lax.fori_loop(0, NI, forward, 0)
@@ -648,45 +719,84 @@
         wait_sends(S.wg.at[l], S.gsend.at[l], nd - 1)
 
     S.F[R_END:, :] = jnp.zeros((nd * rows - R_END, 128), f32)
-    RB = [S.rb0, [S.rb1a, S.rb1b], [S.rb2a, S.rb2b], [S.rb3a, S.rb3b]]
-
-    def recv_of(l):
-        return [S.rr0.at[l], [S.rr1.at[l, c] for c in range(2)], [S.rr2.at[l, c] for c in range(2)], [S.rr3.at[l, c] for c in range(2)]]
+    RB = [
+        [S.rb0.at[l]] + [[getattr(S, "rb%d_%d" % (stage, c)).at[l] for c in range(PARTS)] for stage in (1, 2, 3)]
+        for l in range(L)
+    ]
+    recvs = [
+        [S.rr0.at[l]] + [[ref.at[l, c] for c in range(PARTS)] for ref in (S.rr1, S.rr2, S.rr3)] for l in range(L)
+    ]
+    bounds = [nz * topo[1][0] * topo[2][0], chips_before(topo, rows, R_D), chips_before(topo, rows, R_P), 0]
+    plans = [scatter_plan(net, S.wg.at[l], RB[l], S.rsend.at[l], recvs[l], bounds, 1.2 if l else 0.3) for l in range(L)]
 
     def total(l):
+        for c in range(PARTS):
+            if nz > 1:
+                ref = RB[l][3][c].at[nz - 2]
+                remote(ref, ref, S.rsend.at[l], recvs[l][3][c].at[nz - 2], net.me).wait_recv()
         wait_sends(S.wg.at[l], S.rsend.at[l], nd - 1)
         g = []
-        for c, (first, count) in enumerate(halves(S.wg.shape[2])):
+        for c, (first, count) in enumerate(parts(S.wg.shape[2])):
             part = S.wg[l, net.me, pl.ds(first, count), :].astype(f32)
-            for by in range(nz - 1):
-                part = part + RB[3][c][by].astype(f32)
+            if nz > 1:
+                part = part + RB[l][3][c][nz - 2].astype(f32)
             g.append(part)
         S.vm[:, l, :] = jnp.concatenate(g, axis=0)[0:rows]
 
-    pend, flush = [], nothing
+    queue = []
+    clock = [0.0]
+
+    def add_events(events):
+        queue.extend([clock[0] + event[0]] + event[1:] for event in events)
+        queue.sort(key=lambda event: event[0])
+
+    def due(passed):
+        clock[0] += passed
+        events = []
+        while queue and queue[0][0] <= clock[0]:
+            event = queue.pop(0)
+            events.append(event)
+            for other in queue:
+                if other[2] == event[2] and other[1] > event[1]:
+                    other[0] = max(other[0], clock[0] + AFTER[other[1]] - AFTER[event[1]])
+            queue.sort(key=lambda other: other[0])
+        return events
+
+    def ship(l, w):
+        chips = bounds[w + 1], bounds[w]
+        if chips[0] < chips[1]:
+            pack_and_send(net, S, S.wg.at[l], RB[l], S.rsend.at[l], recvs[l], nd, rows, chips)
+            add_events(plans[l][w])
+
     for l in reversed(range(L)):
-        groups = spread(pend[:-1], 2 * NI)
         S.VG[...] = jnp.zeros_like(S.VG)
-
-        def backward(i, c):
+        groups = [due(1.15) for _ in range(NI)]
+
+        def backward_mlp(i, c):
             bwd_mlp(S, l, i)
-            at_points(groups[0::2], i, flush)
+            at_points(groups, i)
+            return c
+
+        lax.fori_loop(0, NI, backward_mlp, 0)
+        grads_down(S, l)
+        ship(l, 0)
+        run(due(1.8))
+        grads_up(S, l)
+        run(due(1.5))
+        grads_out(S, l)
+        ship(l, 1)
+        run(due(1.3))
+        groups = [due(2.15) for _ in range(NI)]
+
+        def backward_attention(i, c):
             bwd_attention(S, l, i)
-            at_points(groups[1::2], i, flush)
+            at_points(groups, i)
             return c
 
-        lax.fori_loop(0, NI, backward, 0)
-        grads_mlp(S, l)
+        lax.fori_loop(0, NI, backward_attention, 0)
         grads_attention(S, l)
-        if l + 1 < L:
-            pend[-1]()
-            total(l + 1)
-            for peer in peers:
-                pl.semaphore_signal(S.credit, inc=1, device_id=(peer,), device_id_type=pl.DeviceIdType.MESH)
-            pl.semaphore_wait(S.credit, len(peers))
-        recv = recv_of(l)
-        pack_and_send(net, S, S.wg.at[l], RB, S.rsend.at[l], recv, nd, rows)
-        pend, flush = scatter_events(net, S.wg.at[l], RB, S.rsend.at[l], recv)
+        ship(l, 2)
+        run(due(1.6))
 
     def out_tokens(m, c):
         for s in range(slots):
@@ -696,12 +806,17 @@
             S.vdx[m, :, s, :] = S.DX[m * slots + s, 0:SEQ, :]
         return c
 
+    run(due(3.2))
     lax.fori_loop(0, NI // slots, out_tokens, 0)
     outs = [pltpu.make_async_copy(S.vimg, act, S.lsem.at[1]), pltpu.make_async_copy(S.vdx, dimg, S.lsem.at[2])]
     for out in outs:
         out.start()
-    for event in pend:
-        event()
+    for l in range(1, L):
+        total(l)
+    rest = []
+    while queue:
+        rest += due(0.5)
+    run(rest)
     total(0)
     outs.append(pltpu.make_async_copy(S.vm, o_grad, S.lsem.at[0]))
     outs[-1].start()
@@ -712,9 +827,10 @@
 NAMES = (
     ["Wq", "Wp", "Wu", "Wd", "V", "VG", "F", "X", "DX", "DO", "DM", "DA", "DQKV", "wgs"]
     + [name for name, _, _ in SAVED]
-    + ["rb0", "rb1a", "rb1b", "rb2a", "rb2b", "rb3a", "rb3b"]
+    + ["rb0"]
+    + ["rb%d_%d" % (stage, c) for c in range(PARTS) for stage in (1, 2, 3)]
     + ["vm", "vimg", "vcot", "vdx"]
-    + ["lsem", "gsend", "grecv", "rsend", "rr0", "rr1", "rr2", "rr3", "credit"]
+    + ["lsem", "gsend", "grecv", "rsend", "rr0", "rr1", "rr2", "rr3"]
 )
 
 
@@ -726,7 +842,7 @@
     RP = 16 * ((rows + 15) // 16)
     nd = lax.axis_size("fsdp")
     (nz, _), (n1, _), (n2, _), (nc, _) = topo
-    cut = halves(RP)
+    cut = parts(RP)
 
     VM, DMA = pltpu.VMEM, pltpu.SemaphoreType.DMA
     scratch = [
@@ -746,28 +862,26 @@
         VM((L, nd, RP, 128), bf),
     ]
     scratch += [VM((L, NI) + shape, kind) for _, shape, kind in SAVED]
-    scratch += [VM((max(nc - 1, 1), nz * n1 * n2, RP, 128), bf)]
-    scratch += [
-        VM((n2 - 1, nz * n1, cut[0][1], 128), bf),
-        VM((n1 - 1, nz * n2, cut[1][1], 128), bf),
-        VM((n1 - 1, nz, cut[0][1], 128), bf),
-        VM((n2 - 1, nz, cut[1][1], 128), bf),
-        VM((nz - 1, cut[0][1], 128), bf),
-        VM((nz - 1, cut[1][1], 128), bf),
-    ]
+    scratch += [VM((L, max(nc - 1, 1), nz * n1 * n2, RP, 128), bf)]
+    for c in range(PARTS):
+        near, far = ((n2, n1), (n1, n2))[c % 2]
+        scratch += [
+            VM((L, max(near - 1, 1), nz * far, cut[c][1], 128), bf),
+            VM((L, max(far - 1, 1), nz, cut[c][1], 128), bf),
+            VM((L, max(nz - 1, 1), cut[c][1], 128), bf),
+        ]
     tokens = (micro, SEQ, slots, D)
     scratch += [VM((rows, L, 128), f32), VM(tokens, bf), VM(tokens, bf), VM(tokens, f32)]
-    wide_first = max(n1, n2) - 1
+    wide_first = max(n1, n2, 2) - 1
     scratch += [
         DMA((3,)),
         DMA((L,)),
-        DMA((L, 2, nd)),
+        DMA((L, PARTS, nd)),
         DMA((L,)),
         DMA((L, max(nc - 1, 1), nz * n1 * n2)),
-        DMA((L, 2, wide_first, nz * max(n1, n2))),
-        DMA((L, 2, wide_first, nz)),
-        DMA((L, 2, nz - 1)),
-        pltpu.SemaphoreType.REGULAR,
+        DMA((L, PARTS, wide_first, nz * max(n1, n2))),
+        DMA((L, PARTS, wide_first, nz)),
+        DMA((L, PARTS, max(nz - 1, 1))),
     ]
     anywhere = pl.BlockSpec(memory_space=pl.ANY)
     act, grad_in, grad = pl.pallas_call(

time: 140 us -> 135 us (0.964)
  Pallas kernels: 133 us -> 128 us
    pallas_call x1, Pallas kernels: 133 us -> 128 us  [body(): pl.pallas_call(functools.partial(kernel, (topo, L, NI, nd, rows, slots)),...]
where the time goes in v2:
time: 135 us
  Pallas kernels  128 us (95%)
  other arithmetic  4.21 us (3%)
  local copies, waits for them, and re-layouts  2.52 us (2%)
    pallas_call x1, Pallas kernels, body(): pl.pallas_call(functools.partial(kernel, (topo, L, NI, nd, rows, slots)),...  128 us
    sub x1, other arithmetic, body(): new_master = master - learn_rate * (update + decay_rate * master)  4.21 us

profile of v2, /device:TPU:0, one launch (start us, length us, event | category | flops | bytes accessed | tf_op | source)
XLA Modules:
  0.0 134.9 jit_solution(164243741373930920)
XLA Ops:
  0.6 127.6 %step.1 = (bf16[2,197,2,384]{3,2,1,0:T(2,128)(2,1)}, f32[2,197,2,384]{3,2,1,0:T(2,128)}, f32[434,2,128]{2,1,0:T(2,128)}) custom-call(s32[1,2]{1,0:T(1,128)} %bitcast.30, bf16[2,197,2,384]{3,2,1,0:T(2,128)(2,1)} %bitcast.27, bf16[2,197,2,384]{3,2,1,0:T(2,128)(2,1)} %bitcast.28, f32[434,2,128]{2,1,0:T(2,128)} %bitcast.25), custom_call_target="tpu_custom_call" | custom-call | tf_op jit(solution)/shard_map/step/pallas_call | solution.py:887
  128.2 0.0 copy-start.1
  128.2 4.2 %multiply_subtract_fusion = (f32[2,55552]{1,0:T(2,128)}, f32[2,55552]{1,0:T(2,128)}, f32[2,55552]{1,0:T(2,128)}, f32[2,55552]{1,0:T(2,128)}) fusion(f32[2,55552]{1,0:T(2,128)} %param.9, f32[434,2,128]{2,1,0:T(2,128)} %get-tuple-element.11, f32[2,55552]{1,0:T(2,128)} %param.10, f32[2,55552]{1,0:T(2,128)} %param.11), kind=kLoop, calls=%fused_computation.3 | loop fusion | flops 1777664 | bytes 3555328 | tf_op jit(solution)/shard_map/sub | solution.py:909
  132.4 0.0 copy-start
  132.4 0.0 copy-done.1
  132.4 0.8 copy.14
  133.2 0.7 copy-done
  133.9 1.0 copy.15
Async XLA Ops:
  128.2 4.2 %copy-start.1 = (bf16[2,197,2,384]{3,2,1,0:T(2,128)(2,1)S(1)}, bf16[2,197,2,384]{3,2,1,0:T(2,128)(2,1)}, u32[]{:S(2)}) copy-start(bf16[2,197,2,384]{3,2,1,0:T(2,128)(2,1)} %get-tuple-element.9) | copy-start | bytes 1815556
  132.4 1.5 %copy-start = (f32[2,197,2,384]{3,2,1,0:T(2,128)S(1)}, f32[2,197,2,384]{3,2,1,0:T(2,128)}, u32[]{:S(2)}) copy-start(f32[2,197,2,384]{3,2,1,0:T(2,128)} %get-tuple-element.10) | copy-start | bytes 3631108
